TPU v7x, 32 devices: a 4x2x2 block of a 4x4x8 slice. The times are simulated.
32 devices in a mesh: data: 4 (over y, z), tp: 8 (over x, core).
Axes of the slice: x: 4, y: 2, z: 2, core: 2. Of those that a mesh axis runs over, the one named last changes fastest.
The devices are a block of a 4x4x8 slice.
Arguments:
- hidden_acts: bfloat16 [16384, 14336], P('data', 'tp'), parts along dimension 0
- w_down: bfloat16 [14336, 3584], P('tp')
- w_next: bfloat16 [3584, 8192], P(None, 'tp')
Outputs:
- output: bfloat16 [16384, 8192], P('data', 'tp'), parts along dimension 0
There are 4 independent parts. A program takes and returns all parts, laid end to end along the dimension named above; an argument that names none is the same for every part.
All inputs are finite; a program needn't handle non-finite values.
Results may differ from a plain program's by a relative error of at most 0.00114.
Values are sent between devices in bfloat16 or wider.
A program may use at most 768 MiB of HBM per device.

v0:
```python
import jax
import jax.numpy as jnp
from jax import lax
from jax.sharding import PartitionSpec as P, NamedSharding


def solution(mesh):
    def local_step(acts_blk, down_blk, next_blk):
        part_prod = jnp.dot(acts_blk, down_blk, preferred_element_type=jnp.float32)
        row_sum = lax.psum_scatter(part_prod, "tp", scatter_dimension=0, tiled=True)
        row_block = row_sum.astype(jnp.bfloat16)
        mixed = lax.all_gather(row_block, "tp", axis=0, tiled=True)
        return jnp.dot(mixed, next_blk, preferred_element_type=jnp.float32).astype(jnp.bfloat16)

    return jax.shard_map(local_step, mesh=mesh, in_specs=(P("data", "tp"), P("tp", None), P(None, "tp")), out_specs=P("data", "tp"), check_vma=False)
```

profile of v0, /device:TPU:81, one launch (start us, length us, event | category | flops | bytes accessed | tf_op | source)
XLA Modules:
  0.0 545.0 jit_solution(9292781685125603338)
XLA Ops:
  6.5 0.0 reduce-scatter.2.cloned.1.call-start
  6.6 62.8 %fusion = f32[4096,3584]{1,0:T(8,128)} fusion(bf16[4096,1792]{1,0:T(8,128)(2,1)} %param.3, bf16[1792,3584]{1,0:T(8,128)(2,1)} %param.4), kind=kOutput, calls=%fused_computation.1 | convolution fusion | flops 52613349376 | bytes 86245376 | tf_op jit(solution)/shard_map/dot_general | solution.py:9
  69.4 0.1 reduce-scatter.2.cloned.1.call-update
  69.5 0.2 all-gather.2.cloned.1.call-start
  69.7 289.4 %reduce-scatter.2.cloned.1.call-done = f32[512,3584]{1,0:T(8,128)} async-done(((f32[4096,3584]{1,0:T(8,128)}), f32[512,3584]{1,0:T(8,128)}) %reduce-scatter.2.cloned.1.call-update) | async-done | bytes 7340048 | tf_op jit(solution)/shard_map/reduce_scatter | solution.py:10
  359.1 5.3 convert_element_type.6
  364.4 0.1 all-gather.2.cloned.1.call-update
  364.4 136.4 %all-gather.2.cloned.1.call-done = bf16[4096,3584]{1,0:T(8,128)(2,1)} async-done(((bf16[512,3584]{1,0:T(8,128)(2,1)}), bf16[4096,3584]{1,0:T(8,128)(2,1)}) %all-gather.2.cloned.1.call-update) | async-done | bytes 29360144 | tf_op jit(solution)/shard_map/all_gather | solution.py:12
  500.8 37.3 %convolution_convert_fusion = bf16[4096,1024]{1,0:T(8,128)(2,1)} fusion(bf16[4096,3584]{1,0:T(8,128)(2,1)} %all-gather.2.cloned.1.call-done, bf16[3584,1024]{1,0:T(8,128)(2,1)} %param.5), kind=kOutput, calls=%fused_computation | convolution fusion | flops 30068965376 | bytes 45088768 | tf_op jit(solution)/shard_map/dot_general | solution.py:13
Async XLA Ops:
  6.5 352.5 %reduce-scatter.2.cloned.1.call-start = ((), (), s32[]{:S(2)}) async-start(), calls=%async_computation.1 | async-start | bytes 66060288 | tf_op jit(solution)/shard_map/reduce_scatter | solution.py:10
  69.5 431.3 %all-gather.2.cloned.1.call-start = ((), (), s32[]{:S(2)}) async-start(), calls=%async_computation.2 | async-start | bytes 33030144 | tf_op jit(solution)/shard_map/all_gather | solution.py:12
Sparse Core Ops, SparseCore 0:
  69.6 289.4 reduce-scatter.1
  364.6 136.1 all-gather.1
where the time goes:
time: 545 us
  waiting for transfers between devices  426 us (78%)
  matrix products  100 us (18%)
  between operations  13.4 us (2%)
    reduce_scatter x1, waiting for transfers between devices, local_step(): row_sum = lax.psum_scatter(part_prod, 'tp', scatter_dimension=0, tiled=True)  289 us
    all_gather x1, waiting for transfers between devices, local_step(): mixed = lax.all_gather(row_block, 'tp', axis=0, tiled=True)  136 us
    dot_general x1, matrix products, local_step(): part_prod = jnp.dot(acts_blk, down_blk, preferred_element_type=jnp.float32)  62.8 us
    dot_general x1, matrix products, local_step(): jnp.dot(mixed, next_blk, preferred_element_type=jnp.float32)  37.3 us
  transfers between devices with their start and end apart: 2, of which 2 were waited for; matrix products, arithmetic and copies ran while one was open for 0% of the time, Pallas kernels for 0%

commit v1 on v0

v1 whole, which is shorter than its diff:
```python
import functools

import jax
import jax.numpy as jnp
from jax import lax
from jax.experimental import pallas as pl
from jax.experimental.pallas import tpu as pltpu
from jax.sharding import PartitionSpec as P

MESH = pl.DeviceIdType.MESH
UNIT = 32
P_SLOTS, D_SLOTS, HOP_SLOTS, ROOT_SLOTS, Y_SLOTS = 3, 2, 4, 4, 6
PLUS, MINUS = 0, 1


def kernel(ring, rounds, x_hbm, w_hbm, v_hbm, u_hbm, w_vm, v_vm, x_vm, part, pair, hop, root, y_vm, u_vm,
           w_sem, v_sem, x_sem, u_sem, pair_send, pair_recv, hop_send, hop_recv, dir_send, dir_recv, fwd_send, fwd_recv,
           ag_send, ag_recv, agf_send, agf_recv, yp_send, yp_recv):
    width = w_hbm.shape[1]
    half = width // 2
    rows = x_vm.shape[1]
    me = lax.axis_index("tp")
    chip, core = me // 2, lax.rem(me, 2)
    right, left, far = lax.rem(chip + 1, ring), lax.rem(chip + ring - 1, ring), lax.rem(chip + 2, ring)
    partner = {"tp": chip * 2 + 1 - core}
    to = ({"tp": right * 2 + core}, {"tp": left * 2 + core})
    mine, theirs = core * ring, (1 - core) * ring
    cols = (pl.ds(0, half), pl.ds(half, half))

    def remote(src, dst, send, recv, where):
        return pltpu.make_async_remote_copy(src_ref=src, dst_ref=dst, send_sem=send, recv_sem=recv, device_id=where, device_id_type=MESH)

    def load_x(k):
        return pltpu.make_async_copy(x_hbm.at[pl.ds(k * rows, rows)], x_vm.at[lax.rem(k, 2)], x_sem.at[lax.rem(k, 2)])

    def load_w(h):
        return pltpu.make_async_copy(w_hbm.at[:, cols[h]], w_vm.at[:, cols[h]], w_sem.at[h])

    def load_v():
        return pltpu.make_async_copy(v_hbm, v_vm, v_sem)

    def store_u(k):
        return pltpu.make_async_copy(u_vm.at[lax.rem(k, 2)], u_hbm.at[pl.ds(k * rows, rows)], u_sem.at[lax.rem(k, 2)])

    def pair_copy(k, h):
        s, d = lax.rem(k, P_SLOTS), lax.rem(k, D_SLOTS)
        return remote(part.at[s, pl.ds(theirs, ring), :, cols[h]], pair.at[d, :, :, cols[h]], pair_send.at[s, h], pair_recv.at[d, h], partner)

    def hop_copy(k, d):
        s, t = lax.rem(k, P_SLOTS), lax.rem(k, HOP_SLOTS)
        return remote(part.at[s, mine + far, :, cols[d]], hop.at[t, d], hop_send.at[s, d], hop_recv.at[t, d], to[d])

    def dir_copy(k, d):
        s, t = lax.rem(k, P_SLOTS), lax.rem(k, ROOT_SLOTS)
        unit = right if d == PLUS else left
        return remote(part.at[s, mine + unit, :, cols[1 - d]], root.at[t, d, 1 - d], dir_send.at[s, d], dir_recv.at[t, d], to[d])

    def fwd_copy(k, d):
        s, t = lax.rem(k, P_SLOTS), lax.rem(k, ROOT_SLOTS)
        unit = right if d == PLUS else left
        return remote(part.at[s, mine + unit, :, cols[d]], root.at[t, d, d], fwd_send.at[s, d], fwd_recv.at[t, d], to[d])

    def ag_copy(k, d):
        t = lax.rem(k, Y_SLOTS)
        ref = y_vm.at[t, mine + chip]
        return remote(ref, ref, ag_send.at[t, d], ag_recv.at[t, d], to[d])

    def agf_copy(k, d):
        t = lax.rem(k, Y_SLOTS)
        unit = left if d == PLUS else right
        ref = y_vm.at[t, mine + unit, :, cols[d]]
        return remote(ref, ref, agf_send.at[t, d], agf_recv.at[t, d], to[d])

    def yp_copy(k, unit):
        t = lax.rem(k, Y_SLOTS)
        ref = y_vm.at[t, mine + unit]
        return remote(ref, ref, yp_send.at[t, unit], yp_recv.at[t, unit], partner)

    load_x(0).start()
    load_w(0).start()
    load_w(1).start()
    load_v().start()

    barrier = pltpu.get_barrier_semaphore()
    for other in (partner, *to):
        pl.semaphore_signal(barrier, inc=1, device_id=other, device_id_type=MESH)
    pl.semaphore_wait(barrier, 3)

    def wait_part_sends(k):
        for h in (0, 1):
            pair_copy(k, h).wait_send()
            hop_copy(k, h).wait_send()
            dir_copy(k, h).wait_send()
            fwd_copy(k, h).wait_send()

    def product(k):
        load_x(k).wait()

        @pl.when(k + 1 < rounds)
        def _():
            load_x(k + 1).start()

        @pl.when(k >= P_SLOTS)
        def _():
            wait_part_sends(k - P_SLOTS)

        s = lax.rem(k, P_SLOTS)
        for h in (0, 1):
            @pl.when(k == 0)
            def _():
                load_w(h).wait()

            acc = jnp.dot(x_vm[lax.rem(k, 2)], w_vm[:, cols[h]], preferred_element_type=jnp.float32)
            part[s, :, :, cols[h]] = acc.reshape(2 * ring, UNIT, half)
            pair_copy(k, h).start()

    def pair_sum(k):
        s, d = lax.rem(k, P_SLOTS), lax.rem(k, D_SLOTS)

        def add(unit, h):
            part[s, mine + unit, :, cols[h]] += pair[d, unit, :, cols[h]]

        pair_copy(k, 0).wait_recv()
        add(far, 0)
        hop_copy(k, PLUS).start()
        pair_copy(k, 1).wait_recv()
        add(far, 1)
        hop_copy(k, MINUS).start()
        add(right, 1)
        dir_copy(k, PLUS).start()
        add(left, 0)
        dir_copy(k, MINUS).start()
        add(right, 0)
        add(left, 1)
        add(chip, 0)
        add(chip, 1)

    def relay(k):
        s, t = lax.rem(k, P_SLOTS), lax.rem(k, HOP_SLOTS)
        for d in (PLUS, MINUS):
            unit = right if d == PLUS else left
            hop_copy(k, d).wait_recv()
            part[s, mine + unit, :, cols[d]] += hop[t, d]
            fwd_copy(k, d).start()

    def finish(k):
        s, t, y = lax.rem(k, P_SLOTS), lax.rem(k, ROOT_SLOTS), lax.rem(k, Y_SLOTS)
        for d in (PLUS, MINUS):
            dir_copy(k, d).wait_recv()
            fwd_copy(k, d).wait_recv()
        for h in (0, 1):
            total = part[s, mine + chip, :, cols[h]] + root[t, PLUS, h] + root[t, MINUS, h]
            y_vm[y, mine + chip, :, cols[h]] = total.astype(jnp.bfloat16)
        for d in (PLUS, MINUS):
            ag_copy(k, d).start()
        yp_copy(k, chip).start()

    def spread(k):
        for d in (PLUS, MINUS):
            ag_copy(k, d).wait_recv()
            agf_copy(k, d).start()
        yp_copy(k, left).start()
        yp_copy(k, right).start()

    def share(k):
        for d in (PLUS, MINUS):
            agf_copy(k, d).wait_recv()
        yp_copy(k, far).start()

    def project(k):
        y = lax.rem(k, Y_SLOTS)
        for unit in range(ring):
            yp_copy(k, unit).wait_recv()
        for d in (PLUS, MINUS):
            ag_copy(k, d).wait_send()
            agf_copy(k, d).wait_send()
        for unit in range(ring):
            yp_copy(k, unit).wait_send()

        @pl.when(k == 0)
        def _():
            load_v().wait()

        @pl.when(k >= 2)
        def _():
            store_u(k - 2).wait()

        full = y_vm[y].reshape(rows, width)
        u_vm[lax.rem(k, 2)] = jnp.dot(full, v_vm[...], preferred_element_type=jnp.float32).astype(jnp.bfloat16)
        store_u(k).start()

    def step(i, carry):
        for stage, lag in ((product, 0), (project, 5), (pair_sum, 0), (relay, 1), (finish, 2), (spread, 3), (share, 4)):
            k = i - lag

            @pl.when(jnp.logical_and(k >= 0, k < rounds))
            def _():
                stage(k)

        return carry

    lax.fori_loop(0, rounds + 5, step, 0)
    for k in range(rounds - P_SLOTS, rounds):
        wait_part_sends(k)
    for k in range(rounds - 2, rounds):
        store_u(k).wait()


def solution(mesh):
    ring = mesh.shape["tp"] // 2

    def local_step(x, w, v):
        tokens, depth = x.shape
        width, out = v.shape
        rows = 2 * ring * UNIT
        rounds = tokens // rows
        half = width // 2
        dma = pltpu.SemaphoreType.DMA
        f32, bf16 = jnp.float32, jnp.bfloat16
        any_spec = pl.BlockSpec(memory_space=pl.ANY)
        return pl.pallas_call(
            functools.partial(kernel, ring, rounds),
            out_shape=jax.ShapeDtypeStruct((tokens, out), bf16),
            in_specs=[any_spec] * 3,
            out_specs=any_spec,
            scratch_shapes=[
                pltpu.VMEM((depth, width), bf16),
                pltpu.VMEM((width, out), bf16),
                pltpu.VMEM((2, rows, depth), bf16),
                pltpu.VMEM((P_SLOTS, 2 * ring, UNIT, width), f32),
                pltpu.VMEM((D_SLOTS, ring, UNIT, width), f32),
                pltpu.VMEM((HOP_SLOTS, 2, UNIT, half), f32),
                pltpu.VMEM((ROOT_SLOTS, 2, 2, UNIT, half), f32),
                pltpu.VMEM((Y_SLOTS, 2 * ring, UNIT, width), bf16),
                pltpu.VMEM((2, rows, out), bf16),
                dma((2,)), dma, dma((2,)), dma((2,)),
                dma((P_SLOTS, 2)), dma((D_SLOTS, 2)),
                dma((P_SLOTS, 2)), dma((HOP_SLOTS, 2)),
                dma((P_SLOTS, 2)), dma((ROOT_SLOTS, 2)),
                dma((P_SLOTS, 2)), dma((ROOT_SLOTS, 2)),
                dma((Y_SLOTS, 2)), dma((Y_SLOTS, 2)),
                dma((Y_SLOTS, 2)), dma((Y_SLOTS, 2)),
                dma((Y_SLOTS, ring)), dma((Y_SLOTS, ring)),
            ],
            compiler_params=pltpu.CompilerParams(collective_id=0, has_side_effects=True, vmem_limit_bytes=67_043_328),
            cost_estimate=pl.CostEstimate(flops=2 * tokens * (depth * width + width * out), bytes_accessed=2 * (tokens * depth + depth * width + width * out + tokens * out), transcendentals=0),
        )(x, w, v)

    return jax.shard_map(local_step, mesh=mesh, in_specs=(P("data", "tp"), P("tp", None), P(None, "tp")), out_specs=P("data", "tp"), check_vma=False)
```

time: 545 us -> 381 us (0.70)
  waiting for transfers between devices: 426 us -> 0 us
  Pallas kernels: 0 us -> 374 us
  matrix products: 100 us -> 0 us
  between operations: 13.4 us -> 0.01 us
  local copies, waits for them, and re-layouts: 0 us -> 7.76 us
    pallas_call x0 -> x1, Pallas kernels: none -> 374 us  [local_step(): pl.pallas_call(functools.partial(kernel, ring, rounds), out_shape=jax.Sha...]
    reduce_scatter x1 -> x0, waiting for transfers between devices: 289 us -> none  [local_step(): row_sum = lax.psum_scatter(part_prod, 'tp', scatter_dimension=0, tiled=True)]
    all_gather x1 -> x0, waiting for transfers between devices: 136 us -> none  [local_step(): mixed = lax.all_gather(row_block, 'tp', axis=0, tiled=True)]
    dot_general x2 -> x0, matrix products: 100 us -> none  [the longest x1 62.8 us: local_step(): part_prod = jnp.dot(acts_blk, down_blk, preferred_element_type=jnp.float32)]
    unnamed x0 -> x1, local copies, waits for them, and re-layouts: none -> 7.76 us
  transfers between devices with their start and end apart: 2 -> 0, of which waited for: 2 -> 0; matrix products, arithmetic and copies ran while one was open for 0% -> 0% of each run, Pallas kernels for 0% -> 0%
where the time goes in v1:
time: 381 us
  Pallas kernels  374 us (98%)
  local copies, waits for them, and re-layouts  7.76 us (2%)
    pallas_call x1, Pallas kernels, local_step(): pl.pallas_call(functools.partial(kernel, ring, rounds), out_shape=jax.Sha...  374 us
    unnamed x1, local copies, waits for them, and re-layouts  7.76 us

profile of v1, /device:TPU:81, one launch (start us, length us, event | category | flops | bytes accessed | tf_op | source)
XLA Modules:
  0.0 381.3 jit_solution(17926058702540692749)
XLA Ops:
  0.0 373.5 %shard_map.37 = bf16[4096,1024]{1,0:T(8,128)(2,1)} custom-call(bf16[4096,1792]{1,0:T(8,128)(2,1)} %x_hbm.1, bf16[1792,3584]{1,0:T(8,128)(2,1)} %w_hbm.1, bf16[3584,1024]{1,0:T(8,128)(2,1)} %v_hbm.1), custom_call_target="tpu_custom_call" | custom-call | flops 82678120448 | bytes 43253760 | tf_op jit(solution)/shard_map/pallas_call | solution.py:221
  373.6 7.8 %copy.5 = bf16[4096,1024]{1,0:T(8,128)(2,1)} copy(bf16[4096,1024]{1,0:T(8,128)(2,1)} %shard_map.37) | data formatting | bytes 16777216

commit v2 on v0

v2 whole, which is shorter than its diff:
```python
import functools

import jax
import jax.numpy as jnp
from jax import lax
from jax.experimental import pallas as pl
from jax.experimental.pallas import tpu as pltpu
from jax.sharding import PartitionSpec as P

MESH = pl.DeviceIdType.MESH
UNIT = 16
TAIL = 2
P_SLOTS, D_SLOTS, HOP_SLOTS, ROOT_SLOTS, Y_SLOTS, G_SLOTS = 3, 2, 4, 4, 6, 4
PLUS, MINUS = 0, 1
WIDE, LAG, AHEAD = 512, 2, 3


def first_blocks(half):
    starts = [0, *range(half % WIDE, half, WIDE)] if half % WIDE else list(range(0, half, WIDE))
    return [(side, c, d - c) for c, d in zip(starts, starts[1:] + [half]) for side in (PLUS, MINUS)]


def reduce_and_project(ring, rounds, x_hbm, w_hbm, v_hbm, u_vm, v_vm, y_last, w_vm, x_vm, part, pair, hop, root, y_vm,
                       w_sem, v_sem, x_sem, part_send, pair_recv, first_pair, first_hop, hop_recv, root_recv,
                       y_send, ag_recv, agf_recv, yp_recv):
    width = w_hbm.shape[1]
    half = width // 2
    rows = x_vm.shape[1]
    me = lax.axis_index("tp")
    chip, core = me // 2, lax.rem(me, 2)
    right, left, far = lax.rem(chip + 1, ring), lax.rem(chip + ring - 1, ring), lax.rem(chip + 2, ring)
    partner = {"tp": chip * 2 + 1 - core}
    to = ({"tp": right * 2 + core}, {"tp": left * 2 + core})
    next_unit = (right, left)
    mine, theirs = core * ring, (1 - core) * ring
    cols = (pl.ds(0, half), pl.ds(half, half))
    blocks = first_blocks(half)

    def remote(src, dst, send, recv, where):
        return pltpu.make_async_remote_copy(src_ref=src, dst_ref=dst, send_sem=send, recv_sem=recv, device_id=where, device_id_type=MESH)

    def await_bytes(ref, sem):
        pltpu.make_async_copy(ref, ref, sem).wait()

    def fine(b):
        side, start, size = blocks[b]
        return pl.ds(side * half + start, size)

    def load_x(k):
        return pltpu.make_async_copy(x_hbm.at[pl.ds(k * rows, rows)], x_vm.at[lax.rem(k, 2)], x_sem.at[lax.rem(k, 2)])

    def load_w(b):
        return pltpu.make_async_copy(w_hbm.at[:, fine(b)], w_vm.at[:, fine(b)], w_sem.at[b])

    def load_v():
        return pltpu.make_async_copy(v_hbm, v_vm, v_sem)

    def pair_copy(k, h):
        s, d = lax.rem(k, P_SLOTS), lax.rem(k, D_SLOTS)
        return remote(part.at[s, pl.ds(theirs, ring), :, cols[h]], pair.at[d, :, :, cols[h]], part_send.at[s], pair_recv.at[d, h], partner)

    def hop_copy(k, d):
        s, t = lax.rem(k, P_SLOTS), lax.rem(k, HOP_SLOTS)
        return remote(part.at[s, mine + far, :, cols[d]], hop.at[t, d], part_send.at[s], hop_recv.at[t, d], to[d])

    def to_root(k, d, h):
        s, t = lax.rem(k, P_SLOTS), lax.rem(k, ROOT_SLOTS)
        return remote(part.at[s, mine + next_unit[d], :, cols[h]], root.at[t, d, h], part_send.at[s], root_recv.at[t], to[d])

    def ag_copy(k, d, h):
        t, g = lax.rem(k, Y_SLOTS), lax.rem(k, G_SLOTS)
        ref = y_vm.at[t, mine + chip, :, cols[h]]
        return remote(ref, ref, y_send.at[t], ag_recv.at[g, d, h], to[d])

    def agf_copy(k, d):
        t, g = lax.rem(k, Y_SLOTS), lax.rem(k, G_SLOTS)
        ref = y_vm.at[t, mine + next_unit[1 - d], :, cols[d]]
        return remote(ref, ref, y_send.at[t], agf_recv.at[g], to[d])

    def yp_copy(k, unit):
        t = lax.rem(k, Y_SLOTS)
        ref = y_vm.at[t, mine + unit]
        return remote(ref, ref, y_send.at[t], yp_recv.at[t], partner)

    def wait_part_sends(k):
        s = lax.rem(k, P_SLOTS)
        await_bytes(part.at[s, pl.ds(0, ring + 3)], part_send.at[s])

    def product_half(k, h):
        s = lax.rem(k, P_SLOTS)
        acc = jnp.dot(x_vm[lax.rem(k, 2)], w_vm[:, cols[h]], preferred_element_type=jnp.float32)
        part[s, :, :, cols[h]] = acc.reshape(2 * ring, UNIT, half)
        pair_copy(k, h).start()

    def product(k):
        load_x(k).wait()

        @pl.when(k + 1 < rounds)
        def _():
            load_x(k + 1).start()

        @pl.when(k >= P_SLOTS)
        def _():
            wait_part_sends(k - P_SLOTS)

        product_half(k, 0)
        product_half(k, 1)

    def add_pair(k, unit, h):
        s, d = lax.rem(k, P_SLOTS), lax.rem(k, D_SLOTS)
        part[s, mine + unit, :, cols[h]] += pair[d, unit, :, cols[h]]

    def pair_far(k, h):
        pair_copy(k, h).wait_recv()
        add_pair(k, far, h)
        hop_copy(k, h).start()

    def pair_rest(k):
        for d in (PLUS, MINUS):
            add_pair(k, next_unit[d], 1 - d)
            to_root(k, d, 1 - d).start()
        for d in (PLUS, MINUS):
            add_pair(k, next_unit[d], d)
        for h in (0, 1):
            add_pair(k, chip, h)

    def pair_sum(k):
        pair_far(k, 0)
        pair_far(k, 1)
        pair_rest(k)

    def relay(k):
        s, t = lax.rem(k, P_SLOTS), lax.rem(k, HOP_SLOTS)
        for d in (PLUS, MINUS):
            hop_copy(k, d).wait_recv()
            part[s, mine + next_unit[d], :, cols[d]] += hop[t, d]
            to_root(k, d, d).start()

    def finish(k):
        s, t, y = lax.rem(k, P_SLOTS), lax.rem(k, ROOT_SLOTS), lax.rem(k, Y_SLOTS)
        await_bytes(root.at[t], root_recv.at[t])
        for h in (0, 1):
            total = part[s, mine + chip, :, cols[h]] + root[t, PLUS, h] + root[t, MINUS, h]
            y_vm[y, mine + chip, :, cols[h]] = total.astype(jnp.bfloat16)
        for d in (PLUS, MINUS):
            ag_copy(k, d, d).start()
        for d in (PLUS, MINUS):
            ag_copy(k, d, 1 - d).start()
        yp_copy(k, chip).start()

    def spread(k):
        for d in (PLUS, MINUS):
            ag_copy(k, d, d).wait_recv()
            agf_copy(k, d).start()
        for d in (PLUS, MINUS):
            ag_copy(k, d, 1 - d).wait_recv()
            yp_copy(k, next_unit[1 - d]).start()

    def share(k):
        t, g = lax.rem(k, Y_SLOTS), lax.rem(k, G_SLOTS)
        await_bytes(y_vm.at[t, mine + far], agf_recv.at[g])
        yp_copy(k, far).start()

    def project(k):
        y = lax.rem(k, Y_SLOTS)
        await_bytes(y_vm.at[y, pl.ds(0, ring)], yp_recv.at[y])
        await_bytes(y_vm.at[y, pl.ds(0, ring + 3)], y_send.at[y])

        @pl.when(k == 0)
        def _():
            load_v().wait()

        @pl.when(k < rounds - TAIL)
        def _():
            full = y_vm[y].reshape(rows, width)
            u_vm[pl.ds(pl.multiple_of(k * rows, rows), rows)] = jnp.dot(full, v_vm[...], preferred_element_type=jnp.float32).astype(jnp.bfloat16)

        for n in range(TAIL):
            @pl.when(k == rounds - TAIL + n)
            def _():
                y_last[pl.ds(n * rows, rows)] = y_vm[y].reshape(rows, width)

    def first_rounds():
        def pair_fine(b):
            return remote(part.at[0, pl.ds(theirs, ring), :, fine(b)], pair.at[0, :, :, fine(b)], part_send.at[0], first_pair.at[b], partner)

        def make(b):
            load_w(b).wait()
            if b + AHEAD < len(blocks):
                load_w(b + AHEAD).start()
            acc = jnp.dot(x_vm[0], w_vm[:, fine(b)], preferred_element_type=jnp.float32)
            part[0, :, :, fine(b)] = acc.reshape(2 * ring, UNIT, acc.shape[1])
            if b == 0:
                pl.semaphore_wait(barrier, 3)
            pair_fine(b).start()

        def send(b):
            d, start, size = blocks[b]
            within = pl.ds(start, size)
            pair_fine(b).wait_recv()
            part[0, pl.ds(mine, ring), :, fine(b)] += pair[0, :, :, fine(b)]
            remote(part.at[0, mine + far, :, fine(b)], hop.at[0, d, :, within], part_send.at[0], first_hop.at[b], to[d]).start()
            e = 1 - d
            remote(part.at[0, mine + next_unit[e], :, fine(b)], root.at[0, e, d, :, within], part_send.at[0], root_recv.at[0], to[e]).start()

        def pass_on(*which):
            for b in which:
                d, start, size = blocks[b]
                within = pl.ds(start, size)
                await_bytes(hop.at[0, d, :, within], first_hop.at[b])
                part[0, mine + next_unit[d], :, fine(b)] += hop[0, d, :, within]
                remote(part.at[0, mine + next_unit[d], :, fine(b)], root.at[0, d, d, :, within], part_send.at[0], root_recv.at[0], to[d]).start()

        count = len(blocks)
        load_x(0).wait()
        load_x(1).start()
        for b in range(count + LAG):
            if b < count:
                make(b)
            if b >= LAG:
                send(b - LAG)
        pass_on(*range(count - 5))
        load_x(1).wait()
        load_x(2).start()
        product_half(1, 0)
        pass_on(*range(count - 5, count - 3))
        product_half(1, 1)
        pass_on(*range(count - 3, count - 1))
        pair_far(1, 0)
        pass_on(count - 1)
        pair_far(1, 1)
        pair_rest(1)
        load_v().start()

    load_x(0).start()
    for b in range(AHEAD):
        load_w(b).start()
    barrier = pltpu.get_barrier_semaphore()
    for other in (partner, *to):
        pl.semaphore_signal(barrier, inc=1, device_id=other, device_id_type=MESH)
    first_rounds()

    def step(i, carry):
        for stage, lag in ((product, 0), (pair_sum, 0), (relay, 1), (finish, 2), (spread, 3), (share, 4), (project, 5)):
            k = i - lag

            @pl.when(jnp.logical_and(k >= 0, k < rounds))
            def _():
                stage(k)

        return carry

    lax.fori_loop(2, rounds + 5, step, 0)
    for k in range(rounds - P_SLOTS, rounds):
        wait_part_sends(k)


def write_out(y_last, v_vm, u_vm, u_hbm, tail, sem):
    tokens, rows = u_vm.shape[0], y_last.shape[0]
    done = pl.ds(0, tokens - rows)
    early = pltpu.make_async_copy(u_vm.at[done], u_hbm.at[done], sem.at[0])
    late = pltpu.make_async_copy(tail, u_hbm.at[pl.ds(tokens - rows, rows)], sem.at[1])
    early.start()
    tail[...] = jnp.dot(y_last[...], v_vm[...], preferred_element_type=jnp.float32).astype(jnp.bfloat16)
    late.start()
    early.wait()
    late.wait()


def solution(mesh):
    ring = mesh.shape["tp"] // 2

    def local_step(x, w, v):
        tokens, depth = x.shape
        width, out = v.shape
        rows = 2 * ring * UNIT
        rounds = tokens // rows
        half = width // 2
        count = len(first_blocks(half))
        dma = pltpu.SemaphoreType.DMA
        f32, bf16 = jnp.float32, jnp.bfloat16
        any_spec = pl.BlockSpec(memory_space=pl.ANY)
        vmem_spec = pl.BlockSpec(memory_space=pltpu.VMEM)
        u, v_kept, y_last = pl.pallas_call(
            functools.partial(reduce_and_project, ring, rounds),
            out_shape=[pltpu.VMEM((tokens, out), bf16), pltpu.VMEM((width, out), bf16), pltpu.VMEM((TAIL * rows, width), bf16)],
            in_specs=[any_spec] * 3,
            out_specs=[vmem_spec] * 3,
            scratch_shapes=[
                pltpu.VMEM((depth, width), bf16),
                pltpu.VMEM((2, rows, depth), bf16),
                pltpu.VMEM((P_SLOTS, 2 * ring, UNIT, width), f32),
                pltpu.VMEM((D_SLOTS, ring, UNIT, width), f32),
                pltpu.VMEM((HOP_SLOTS, 2, UNIT, half), f32),
                pltpu.VMEM((ROOT_SLOTS, 2, 2, UNIT, half), f32),
                pltpu.VMEM((Y_SLOTS, 2 * ring, UNIT, width), bf16),
                dma((count,)), dma, dma((2,)),
                dma((P_SLOTS,)), dma((D_SLOTS, 2)), dma((count,)), dma((count,)), dma((HOP_SLOTS, 2)), dma((ROOT_SLOTS,)),
                dma((Y_SLOTS,)), dma((G_SLOTS, 2, 2)), dma((G_SLOTS,)), dma((Y_SLOTS,)),
            ],
            compiler_params=pltpu.CompilerParams(collective_id=0, has_side_effects=True, vmem_limit_bytes=40_000_000),
            cost_estimate=pl.CostEstimate(flops=2 * tokens * (depth * width + width * out), bytes_accessed=2 * (tokens * depth + depth * width + width * out), transcendentals=0),
        )(x, w, v)
        return pl.pallas_call(
            write_out,
            out_shape=jax.ShapeDtypeStruct((tokens, out), bf16),
            in_specs=[vmem_spec] * 3,
            out_specs=any_spec,
            scratch_shapes=[pltpu.VMEM((TAIL * rows, out), bf16), dma((2,))],
            compiler_params=pltpu.CompilerParams(vmem_limit_bytes=8_000_000),
            cost_estimate=pl.CostEstimate(flops=2 * TAIL * rows * width * out, bytes_accessed=2 * tokens * out, transcendentals=0),
        )(y_last, v_kept, u)

    return jax.shard_map(local_step, mesh=mesh, in_specs=(P("data", "tp"), P("tp", None), P(None, "tp")), out_specs=P("data", "tp"), check_vma=False)
```

time: 545 us -> 370 us (0.68)
  waiting for transfers between devices: 426 us -> 0 us
  Pallas kernels: 0 us -> 370 us
  matrix products: 100 us -> 0 us
  between operations: 13.4 us -> 0.01 us
    pallas_call x0 -> x2, Pallas kernels: none -> 370 us  [the longest x1 366 us: local_step(): pl.pallas_call(functools.partial(reduce_and_project, ring, rounds), out_s...]
    reduce_scatter x1 -> x0, waiting for transfers between devices: 289 us -> none  [local_step(): row_sum = lax.psum_scatter(part_prod, 'tp', scatter_dimension=0, tiled=True)]
    all_gather x1 -> x0, waiting for transfers between devices: 136 us -> none  [local_step(): mixed = lax.all_gather(row_block, 'tp', axis=0, tiled=True)]
    dot_general x2 -> x0, matrix products: 100 us -> none  [the longest x1 62.8 us: local_step(): part_prod = jnp.dot(acts_blk, down_blk, preferred_element_type=jnp.float32)]
  transfers between devices with their start and end apart: 2 -> 0, of which waited for: 2 -> 0; matrix products, arithmetic and copies ran while one was open for 0% -> 0% of each run, Pallas kernels for 0% -> 0%
where the time goes in v2:
time: 370 us
  Pallas kernels  370 us (100%)
    pallas_call x1, Pallas kernels, local_step(): pl.pallas_call(functools.partial(reduce_and_project, ring, rounds), out_s...  366 us

profile of v2, /device:TPU:81, one launch (start us, length us, event | category | flops | bytes accessed | tf_op | source)
XLA Modules:
  0.0 369.6 jit_solution(5127576356437001819)
XLA Ops:
  0.0 366.2 %shard_map.37 = (bf16[4096,1024]{1,0:T(8,128)(2,1)S(1)}, bf16[3584,1024]{1,0:T(8,128)(2,1)S(1)}, bf16[256,3584]{1,0:T(8,128)(2,1)S(1)}) custom-call(bf16[4096,1792]{1,0:T(8,128)(2,1)} %x_hbm.1, bf16[1792,3584]{1,0:T(8,128)(2,1)} %w_hbm.1, bf16[3584,1024]{1,0:T(8,128)(2,1)} %v_hbm.1), custom_call_target="tpu_custom_call" | custom-call | flops 82678120448 | bytes 34865152 | tf_op jit(solution)/shard_map/pallas_call | solution.py:284
  366.2 3.4 shard_map.38
